TPU v7x, 32 devices: a whole 2x2x4 slice. The times are simulated.
32 devices in a mesh: row: 4 (over z), col: 8 (over y, x, core).
Axes of the slice: x: 2, y: 2, z: 4, core: 2. Of those that a mesh axis runs over, the one named last changes fastest.
Arguments:
- factor_wide: float32 [4, 4, 2, 8, 512, 512], P(None, 'row', None, 'col'), may hold values from -1 to 2, as said below
- factor_narrow: bfloat16 [4, 4, 2, 8, 512, 512], P(None, 'row', None, 'col'), may hold values from -1 to 2, as said below
- flags: int32 [4, 4, 2, 8], P(None, 'row', None, 'col'), may hold values from 0 to 1
- forward_solution: float32 [2, 8, 512, 128], P(None, 'col'), may hold values from -0.5 to 0.5
- solution_grad: float32 [2, 8, 512, 128], P(None, 'col'), may hold values from -1.8 to 1.8
Outputs:
- rhs_grad: float32 [4, 4, 512, 128], P(None, 'row')
- factor_grad: float32 [4, 4, 2, 8, 512, 512], P(None, 'row', None, 'col')
Inputs may be any that keep to these rules, and one draw needn't show every extreme that they name: `factor_wide`: the diagonal entries of every diagonal tile lie between 1 and 2. `factor_narrow`: the diagonal entries of every diagonal tile lie between 1 and 2.
All inputs are finite; a program needn't handle non-finite values.
Results may differ from a plain program's by a relative error of at most 0.0003.
Values sent between devices are 32-bit elements; how exact they have to be, the bound alone decides.
A program may use at most 64 MiB of HBM per device.

v0:
```python
import jax
import jax.numpy as jnp
from jax import lax
from jax.sharding import PartitionSpec as P

HIGHEST_PRECISION = lax.Precision.HIGHEST


def broadcast(value, axis, root):
    mine = lax.axis_index(axis) == root
    return lax.psum(jnp.where(mine, value, jnp.zeros_like(value)), axis)


def from_behind(value, axis, by):
    size = lax.axis_size(axis)
    return lax.ppermute(value, axis, [(i, (i + by) % size) for i in range(size)])


def lower_mask(row_index, col_index, tile_width):
    inner_mask = lax.broadcasted_iota(
        jnp.int32, (tile_width, tile_width), 0
    ) >= lax.broadcasted_iota(jnp.int32, (tile_width, tile_width), 1)
    return (row_index > col_index) | (row_index == col_index) & inner_mask


def body(factor_wide, factor_narrow, flags, forward_solution, solution_grad):
    row_count = lax.axis_size("row")
    col_count = lax.axis_size("col")
    my_row = lax.axis_index("row")
    my_col = lax.axis_index("col")
    local_rows = factor_wide.shape[0]
    local_cols = factor_wide.shape[2]
    tile_width = factor_wide.shape[4]
    rhs_width = forward_solution.shape[3]
    tile_count = local_rows * row_count
    factor_tiles = jnp.where(
        flags[:, 0, :, 0, None, None] == 1,
        factor_narrow[:, 0, :, 0].astype(jnp.float32),
        factor_wide[:, 0, :, 0],
    )
    solution_local = forward_solution[:, 0]
    target_local = solution_grad[:, 0]
    row_index = jnp.arange(local_rows, dtype=jnp.int32) * row_count + my_row
    col_index = jnp.arange(local_cols, dtype=jnp.int32) * col_count + my_col
    empty_block = jnp.zeros((tile_width, rhs_width), jnp.float32)

    def nothing_block():
        return empty_block

    def column_partial(rhs_local, target, lowest):

        def on_owner():
            column = lax.dynamic_index_in_dim(factor_tiles, target // col_count, 1, keepdims=False)
            weight = (row_index >= lowest).astype(jnp.float32)
            masked = rhs_local * weight[:, None, None]
            return jnp.einsum("aki,akr->ir", column, masked, precision=HIGHEST_PRECISION)

        return lax.cond(my_col == target % col_count, on_owner, nothing_block)

    def target_block(target):
        return lax.dynamic_index_in_dim(target_local, target // col_count, 0, keepdims=False)

    def advance(right_side, target, carried):
        rhs_local, factor_grad = carried
        local_slot = target // row_count
        holds_row = my_row == target % row_count
        is_owner = holds_row & (my_col == target % col_count)

        def solve_here():
            tile_row = lax.dynamic_index_in_dim(factor_tiles, local_slot, 0, keepdims=False)
            diagonal = lax.dynamic_index_in_dim(tile_row, target // col_count, 0, keepdims=False)
            return lax.linalg.triangular_solve(
                diagonal, right_side, left_side=True, lower=True, transpose_a=True
            )

        solved = lax.cond(is_owner, solve_here, nothing_block)
        arrived = broadcast(solved, "col", target % col_count)
        current = lax.dynamic_index_in_dim(rhs_local, local_slot, 0, keepdims=False)
        rhs_local = lax.dynamic_update_index_in_dim(
            rhs_local, jnp.where(holds_row, arrived, current), local_slot, 0
        )
        return (rhs_local, factor_grad)

    final_index = tile_count - 1
    carried = (
        jnp.zeros((local_rows, tile_width, rhs_width), jnp.float32),
        jnp.zeros((local_rows, local_cols, tile_width, tile_width), jnp.float32),
    )
    carried = advance(target_block(jnp.int32(final_index)), jnp.int32(final_index), carried)

    def sweep_step(offset, loop_state):
        carried, early_sum = loop_state
        target = final_index - 1 - offset
        rhs_local = carried[0]
        source = target + 1

        def compute_fresh():
            tile_row = lax.dynamic_index_in_dim(
                factor_tiles, source // row_count, 0, keepdims=False
            )
            tile_now = lax.dynamic_index_in_dim(tile_row, target // col_count, 0, keepdims=False)
            newest = lax.dynamic_index_in_dim(rhs_local, source // row_count, 0, keepdims=False)
            return jnp.dot(
                tile_now.T, newest, precision=HIGHEST_PRECISION, preferred_element_type=jnp.float32
            )

        fresh_owner = (my_row == source % row_count) & (my_col == target % col_count)
        fresh_term = lax.cond(fresh_owner, compute_fresh, nothing_block)
        moved_term = from_behind(fresh_term, "row", -1)
        following = jnp.maximum(target - 1, 0)
        next_partial = column_partial(rhs_local, following, source)
        next_sum = lax.psum(next_partial, "row")
        carried = advance(target_block(target) - early_sum - moved_term, target, carried)
        return (carried, next_sum)

    carried, unused_sum = lax.fori_loop(0, final_index, sweep_step, (carried, empty_block))
    rhs_local, factor_grad = carried
    products = -jnp.einsum("akr,blr->abkl", rhs_local, solution_local, precision=HIGHEST_PRECISION)
    masks = lower_mask(row_index[:, None, None, None], col_index[None, :, None, None], tile_width)
    factor_grad = jnp.where(masks, products, jnp.zeros_like(products))
    return (rhs_local[:, None], factor_grad[:, None, :, None])


def solution(mesh):
    placed = (
        P(None, "row", None, "col", None, None),
        P(None, "row", None, "col", None, None),
        P(None, "row", None, "col"),
        P(None, "col", None, None),
        P(None, "col", None, None),
    )
    return jax.shard_map(
        body,
        mesh=mesh,
        in_specs=placed,
        out_specs=(P(None, "row", None, None), P(None, "row", None, "col", None, None)),
        check_vma=False,
    )
```

profile of v0, /device:TPU:0, one launch (start us, length us, event | category | flops | bytes accessed | tf_op | source)
XLA Modules:
  0.0 2219.2 jit_solution(8826648313586827079)
XLA Ops:
  7.3 9.9 copy.12
  17.2 7.3 copy.11
  24.5 9.6 convert_select_fusion
  35.9 117.2 %all-reduce.5.cloned.1.call-done = f32[512,128]{1,0:T(8,128)} async-done(((f32[512,128]{1,0:T(8,128)}), f32[512,128]{1,0:T(8,128)}) %all-reduce.5.cloned.1.call-update) | async-done | bytes 262160 | tf_op jit(solution)/shard_map/psum | solution.py:11
  153.2 2048.1 %while.28 = (s32[]{:T(128)}, f32[4,512,128]{2,1,0:T(8,128)S(1)}, f32[512,128]{1,0:T(8,128)S(1)}, s32[]{:T(128)}, s32[]{:T(128)}, /*index=5*/f32[4,2,512,512]{2,3...) while((s32[]{:T(128)}, f32[4,512,128]{2,1,0:T(8,128)S(1)}, ...), condition=%wide.region_12.14_spmd.clone.clone, body=%wide.region_3.13_spmd.clone.clone.sunk | while | flops 2266480640 | bytes 54005560 | solution.py:116
  163.3 40.6 %all-reduce.9.cloned.1.call-done = f32[512,128]{1,0:T(8,128)} async-done(((f32[512,128]{1,0:T(8,128)}), f32[512,128]{1,0:T(8,128)}) %all-reduce.9.cloned.1.call-update) | async-done | bytes 262160 | tf_op jit(solution)/shard_map/while/body/eval_jaxpr/psum | solution.py:112
  204.9 86.8 %all-reduce.7.cloned.1.call-done = f32[512,128]{1,0:T(8,128)} async-done(((f32[512,128]{1,0:T(8,128)}), f32[512,128]{1,0:T(8,128)}) %all-reduce.7.cloned.1.call-update) | async-done | bytes 262160 | tf_op jit(solution)/shard_map/while/body/eval_jaxpr/psum | solution.py:11
  300.8 39.6 %all-reduce.9.cloned.1.call-done = f32[512,128]{1,0:T(8,128)} async-done(((f32[512,128]{1,0:T(8,128)}), f32[512,128]{1,0:T(8,128)}) %all-reduce.9.cloned.1.call-update) | async-done | bytes 262160 | tf_op jit(solution)/shard_map/while/body/eval_jaxpr/psum | solution.py:112
  341.4 85.4 %all-reduce.7.cloned.1.call-done = f32[512,128]{1,0:T(8,128)} async-done(((f32[512,128]{1,0:T(8,128)}), f32[512,128]{1,0:T(8,128)}) %all-reduce.7.cloned.1.call-update) | async-done | bytes 262160 | tf_op jit(solution)/shard_map/while/body/eval_jaxpr/psum | solution.py:11
  435.9 40.6 %all-reduce.9.cloned.1.call-done = f32[512,128]{1,0:T(8,128)} async-done(((f32[512,128]{1,0:T(8,128)}), f32[512,128]{1,0:T(8,128)}) %all-reduce.9.cloned.1.call-update) | async-done | bytes 262160 | tf_op jit(solution)/shard_map/while/body/eval_jaxpr/psum | solution.py:112
  477.4 85.9 %all-reduce.7.cloned.1.call-done = f32[512,128]{1,0:T(8,128)} async-done(((f32[512,128]{1,0:T(8,128)}), f32[512,128]{1,0:T(8,128)}) %all-reduce.7.cloned.1.call-update) | async-done | bytes 262160 | tf_op jit(solution)/shard_map/while/body/eval_jaxpr/psum | solution.py:11
  572.6 37.7 %all-reduce.9.cloned.1.call-done = f32[512,128]{1,0:T(8,128)} async-done(((f32[512,128]{1,0:T(8,128)}), f32[512,128]{1,0:T(8,128)}) %all-reduce.9.cloned.1.call-update) | async-done | bytes 262160 | tf_op jit(solution)/shard_map/while/body/eval_jaxpr/psum | solution.py:112
  611.3 88.0 %all-reduce.7.cloned.1.call-done = f32[512,128]{1,0:T(8,128)} async-done(((f32[512,128]{1,0:T(8,128)}), f32[512,128]{1,0:T(8,128)}) %all-reduce.7.cloned.1.call-update) | async-done | bytes 262160 | tf_op jit(solution)/shard_map/while/body/eval_jaxpr/psum | solution.py:11
  709.4 40.6 %all-reduce.9.cloned.1.call-done = f32[512,128]{1,0:T(8,128)} async-done(((f32[512,128]{1,0:T(8,128)}), f32[512,128]{1,0:T(8,128)}) %all-reduce.9.cloned.1.call-update) | async-done | bytes 262160 | tf_op jit(solution)/shard_map/while/body/eval_jaxpr/psum | solution.py:112
  751.0 86.8 %all-reduce.7.cloned.1.call-done = f32[512,128]{1,0:T(8,128)} async-done(((f32[512,128]{1,0:T(8,128)}), f32[512,128]{1,0:T(8,128)}) %all-reduce.7.cloned.1.call-update) | async-done | bytes 262160 | tf_op jit(solution)/shard_map/while/body/eval_jaxpr/psum | solution.py:11
  841.4 5.7 conditional.16
  841.4 5.7 fusion.11
  848.8 37.8 %all-reduce.9.cloned.1.call-done = f32[512,128]{1,0:T(8,128)} async-done(((f32[512,128]{1,0:T(8,128)}), f32[512,128]{1,0:T(8,128)}) %all-reduce.9.cloned.1.call-update) | async-done | bytes 262160 | tf_op jit(solution)/shard_map/while/body/eval_jaxpr/psum | solution.py:112
  887.5 85.3 %all-reduce.7.cloned.1.call-done = f32[512,128]{1,0:T(8,128)} async-done(((f32[512,128]{1,0:T(8,128)}), f32[512,128]{1,0:T(8,128)}) %all-reduce.7.cloned.1.call-update) | async-done | bytes 262160 | tf_op jit(solution)/shard_map/while/body/eval_jaxpr/psum | solution.py:11
  977.3 15.6 collective-permute-done
  992.9 65.2 %conditional.15 = (f32[512,128]{1,0:T(8,128)S(1)}) conditional(s32[]{:T(128)} %convert_element_type.68, () %tuple.144, (s32[]{:T(128)}, s32[]{:T(128)}, f32[4,2,512,512]{2,3,0,1:T(8,128)}, s32[]{:T(128)}, pred[]{:T(512)}, /*index=5*/pred[]{:T(512)}, s32[]{:T(128)}, f32[2,512,128]{2,1,0:T(8,128)}, f32[512,128]{1,0:T(8,128)S(1)}, ...), branch_computations={%region_6.7_spmd, %region_7.8_spmd} | conditional | flops 252690464 | bytes 22546512 | solution.py:76
  992.9 10.0 copy.8
  1004.2 10.6 while.27
  1014.8 40.1 %custom-call.5 = f32[4,128,128]{1,2,0:T(8,128)S(1)} custom-call(f32[4,128,128]{2,1,0:T(8,128)} %get-tuple-element.560), custom_call_target="InvertDiagBlocksLowerTriangular" | custom-call | tf_op jit(solution)/shard_map/while/body/eval_jaxpr/cond/branch_1_fun/triangular_solve/custom-call.1 | solution.py:72
  1059.8 48.9 %all-reduce.7.cloned.1.call-done = f32[512,128]{1,0:T(8,128)} async-done(((f32[512,128]{1,0:T(8,128)}), f32[512,128]{1,0:T(8,128)}) %all-reduce.7.cloned.1.call-update) | async-done | bytes 262160 | tf_op jit(solution)/shard_map/while/body/eval_jaxpr/psum | solution.py:11
  1118.0 37.9 %all-reduce.9.cloned.1.call-done = f32[512,128]{1,0:T(8,128)} async-done(((f32[512,128]{1,0:T(8,128)}), f32[512,128]{1,0:T(8,128)}) %all-reduce.9.cloned.1.call-update) | async-done | bytes 262160 | tf_op jit(solution)/shard_map/while/body/eval_jaxpr/psum | solution.py:112
  1156.9 88.0 %all-reduce.7.cloned.1.call-done = f32[512,128]{1,0:T(8,128)} async-done(((f32[512,128]{1,0:T(8,128)}), f32[512,128]{1,0:T(8,128)}) %all-reduce.7.cloned.1.call-update) | async-done | bytes 262160 | tf_op jit(solution)/shard_map/while/body/eval_jaxpr/psum | solution.py:11
  1255.0 40.6 %all-reduce.9.cloned.1.call-done = f32[512,128]{1,0:T(8,128)} async-done(((f32[512,128]{1,0:T(8,128)}), f32[512,128]{1,0:T(8,128)}) %all-reduce.9.cloned.1.call-update) | async-done | bytes 262160 | tf_op jit(solution)/shard_map/while/body/eval_jaxpr/psum | solution.py:112
  1296.5 86.8 %all-reduce.7.cloned.1.call-done = f32[512,128]{1,0:T(8,128)} async-done(((f32[512,128]{1,0:T(8,128)}), f32[512,128]{1,0:T(8,128)}) %all-reduce.7.cloned.1.call-update) | async-done | bytes 262160 | tf_op jit(solution)/shard_map/while/body/eval_jaxpr/psum | solution.py:11
  1392.5 39.6 %all-reduce.9.cloned.1.call-done = f32[512,128]{1,0:T(8,128)} async-done(((f32[512,128]{1,0:T(8,128)}), f32[512,128]{1,0:T(8,128)}) %all-reduce.9.cloned.1.call-update) | async-done | bytes 262160 | tf_op jit(solution)/shard_map/while/body/eval_jaxpr/psum | solution.py:112
  1433.0 85.3 %all-reduce.7.cloned.1.call-done = f32[512,128]{1,0:T(8,128)} async-done(((f32[512,128]{1,0:T(8,128)}), f32[512,128]{1,0:T(8,128)}) %all-reduce.7.cloned.1.call-update) | async-done | bytes 262160 | tf_op jit(solution)/shard_map/while/body/eval_jaxpr/psum | solution.py:11
  1527.5 40.6 %all-reduce.9.cloned.1.call-done = f32[512,128]{1,0:T(8,128)} async-done(((f32[512,128]{1,0:T(8,128)}), f32[512,128]{1,0:T(8,128)}) %all-reduce.9.cloned.1.call-update) | async-done | bytes 262160 | tf_op jit(solution)/shard_map/while/body/eval_jaxpr/psum | solution.py:112
  1569.1 85.9 %all-reduce.7.cloned.1.call-done = f32[512,128]{1,0:T(8,128)} async-done(((f32[512,128]{1,0:T(8,128)}), f32[512,128]{1,0:T(8,128)}) %all-reduce.7.cloned.1.call-update) | async-done | bytes 262160 | tf_op jit(solution)/shard_map/while/body/eval_jaxpr/psum | solution.py:11
  1664.2 37.7 %all-reduce.9.cloned.1.call-done = f32[512,128]{1,0:T(8,128)} async-done(((f32[512,128]{1,0:T(8,128)}), f32[512,128]{1,0:T(8,128)}) %all-reduce.9.cloned.1.call-update) | async-done | bytes 262160 | tf_op jit(solution)/shard_map/while/body/eval_jaxpr/psum | solution.py:112
  1702.9 88.1 %all-reduce.7.cloned.1.call-done = f32[512,128]{1,0:T(8,128)} async-done(((f32[512,128]{1,0:T(8,128)}), f32[512,128]{1,0:T(8,128)}) %all-reduce.7.cloned.1.call-update) | async-done | bytes 262160 | tf_op jit(solution)/shard_map/while/body/eval_jaxpr/psum | solution.py:11
  1801.1 40.6 %all-reduce.9.cloned.1.call-done = f32[512,128]{1,0:T(8,128)} async-done(((f32[512,128]{1,0:T(8,128)}), f32[512,128]{1,0:T(8,128)}) %all-reduce.9.cloned.1.call-update) | async-done | bytes 262160 | tf_op jit(solution)/shard_map/while/body/eval_jaxpr/psum | solution.py:112
  1842.6 86.8 %all-reduce.7.cloned.1.call-done = f32[512,128]{1,0:T(8,128)} async-done(((f32[512,128]{1,0:T(8,128)}), f32[512,128]{1,0:T(8,128)}) %all-reduce.7.cloned.1.call-update) | async-done | bytes 262160 | tf_op jit(solution)/shard_map/while/body/eval_jaxpr/psum | solution.py:11
  1933.0 5.7 conditional.16
  1940.4 37.8 %all-reduce.9.cloned.1.call-done = f32[512,128]{1,0:T(8,128)} async-done(((f32[512,128]{1,0:T(8,128)}), f32[512,128]{1,0:T(8,128)}) %all-reduce.9.cloned.1.call-update) | async-done | bytes 262160 | tf_op jit(solution)/shard_map/while/body/eval_jaxpr/psum | solution.py:112
  1979.1 85.3 %all-reduce.7.cloned.1.call-done = f32[512,128]{1,0:T(8,128)} async-done(((f32[512,128]{1,0:T(8,128)}), f32[512,128]{1,0:T(8,128)}) %all-reduce.7.cloned.1.call-update) | async-done | bytes 262160 | tf_op jit(solution)/shard_map/while/body/eval_jaxpr/psum | solution.py:11
  2068.1 5.7 conditional.16
  2074.6 9.9 collective-permute-done
  2084.6 65.1 %conditional.15 = (f32[512,128]{1,0:T(8,128)S(1)}) conditional(s32[]{:T(128)} %convert_element_type.68, () %tuple.144, (s32[]{:T(128)}, s32[]{:T(128)}, f32[4,2,512,512]{2,3,0,1:T(8,128)}, s32[]{:T(128)}, pred[]{:T(512)}, /*index=5*/pred[]{:T(512)}, s32[]{:T(128)}, f32[2,512,128]{2,1,0:T(8,128)}, f32[512,128]{1,0:T(8,128)S(1)}, ...), branch_computations={%region_6.7_spmd, %region_7.8_spmd} | conditional | flops 252690464 | bytes 22546512 | solution.py:76
  2084.6 10.0 copy.8
  2095.9 10.6 while.27
  2106.5 40.1 %custom-call.5 = f32[4,128,128]{1,2,0:T(8,128)S(1)} custom-call(f32[4,128,128]{2,1,0:T(8,128)} %get-tuple-element.560), custom_call_target="InvertDiagBlocksLowerTriangular" | custom-call | tf_op jit(solution)/shard_map/while/body/eval_jaxpr/cond/branch_1_fun/triangular_solve/custom-call.1 | solution.py:72
  2151.5 48.9 %all-reduce.7.cloned.1.call-done = f32[512,128]{1,0:T(8,128)} async-done(((f32[512,128]{1,0:T(8,128)}), f32[512,128]{1,0:T(8,128)}) %all-reduce.7.cloned.1.call-update) | async-done | bytes 262160 | tf_op jit(solution)/shard_map/while/body/eval_jaxpr/psum | solution.py:11
  2201.4 11.0 fusion.55
  (350 shorter events, 182.1 us)
Async XLA Ops:
  7.2 2194.2 %copy-start = (f32[2,1,512,128]{3,2,1,0:T(8,128)S(1)}, f32[2,1,512,128]{3,2,1,0:T(8,128)}, u32[]{:S(2)}) copy-start(f32[2,1,512,128]{3,2,1,0:T(8,128)} %param.20) | copy-start | bytes 1572868
  7.2 145.9 %all-reduce.5.cloned.1.call-start = ((), (), s32[]{:S(2)}) async-start(), calls=%async_computation | async-start | bytes 524288 | tf_op jit(solution)/shard_map/psum | solution.py:11
  7.2 17.2 copy-start.3
  153.3 50.7 %all-reduce.9.cloned.1.call-start = ((), (), s32[]{:S(2)}) async-start(), calls=%async_computation.2 | async-start | bytes 524288 | tf_op jit(solution)/shard_map/while/body/eval_jaxpr/psum | solution.py:112
  153.4 9.1 collective-permute-start
  158.5 133.2 %all-reduce.7.cloned.1.call-start = ((), (), s32[]{:S(2)}) async-start(), calls=%async_computation.1 | async-start | bytes 524288 | tf_op jit(solution)/shard_map/while/body/eval_jaxpr/psum | solution.py:11
  291.7 48.7 %all-reduce.9.cloned.1.call-start = ((), (), s32[]{:S(2)}) async-start(), calls=%async_computation.2 | async-start | bytes 524288 | tf_op jit(solution)/shard_map/while/body/eval_jaxpr/psum | solution.py:112
  291.9 8.1 collective-permute-start
  296.0 130.7 %all-reduce.7.cloned.1.call-start = ((), (), s32[]{:S(2)}) async-start(), calls=%async_computation.1 | async-start | bytes 524288 | tf_op jit(solution)/shard_map/while/body/eval_jaxpr/psum | solution.py:11
  426.8 49.7 %all-reduce.9.cloned.1.call-start = ((), (), s32[]{:S(2)}) async-start(), calls=%async_computation.2 | async-start | bytes 524288 | tf_op jit(solution)/shard_map/while/body/eval_jaxpr/psum | solution.py:112
  426.9 8.1 collective-permute-start
  431.1 132.2 %all-reduce.7.cloned.1.call-start = ((), (), s32[]{:S(2)}) async-start(), calls=%async_computation.1 | async-start | bytes 524288 | tf_op jit(solution)/shard_map/while/body/eval_jaxpr/psum | solution.py:11
  564.3 46.0 %all-reduce.9.cloned.1.call-start = ((), (), s32[]{:S(2)}) async-start(), calls=%async_computation.2 | async-start | bytes 524288 | tf_op jit(solution)/shard_map/while/body/eval_jaxpr/psum | solution.py:112
  564.5 7.3 collective-permute-start
  567.7 131.6 %all-reduce.7.cloned.1.call-start = ((), (), s32[]{:S(2)}) async-start(), calls=%async_computation.1 | async-start | bytes 524288 | tf_op jit(solution)/shard_map/while/body/eval_jaxpr/psum | solution.py:11
  699.4 50.6 %all-reduce.9.cloned.1.call-start = ((), (), s32[]{:S(2)}) async-start(), calls=%async_computation.2 | async-start | bytes 524288 | tf_op jit(solution)/shard_map/while/body/eval_jaxpr/psum | solution.py:112
  699.5 9.1 collective-permute-start
  704.6 133.1 %all-reduce.7.cloned.1.call-start = ((), (), s32[]{:S(2)}) async-start(), calls=%async_computation.1 | async-start | bytes 524288 | tf_op jit(solution)/shard_map/while/body/eval_jaxpr/psum | solution.py:11
  837.8 48.7 %all-reduce.9.cloned.1.call-start = ((), (), s32[]{:S(2)}) async-start(), calls=%async_computation.2 | async-start | bytes 524288 | tf_op jit(solution)/shard_map/while/body/eval_jaxpr/psum | solution.py:112
  838.0 10.0 collective-permute-start
  847.8 125.0 %all-reduce.7.cloned.1.call-start = ((), (), s32[]{:S(2)}) async-start(), calls=%async_computation.1 | async-start | bytes 524288 | tf_op jit(solution)/shard_map/while/body/eval_jaxpr/psum | solution.py:11
  972.9 86.0 %all-reduce.9.cloned.1.call-start = ((), (), s32[]{:S(2)}) async-start(), calls=%async_computation.2 | async-start | bytes 524288 | tf_op jit(solution)/shard_map/while/body/eval_jaxpr/psum | solution.py:112
  973.0 19.9 collective-permute-start
  977.2 131.5 %all-reduce.7.cloned.1.call-start = ((), (), s32[]{:S(2)}) async-start(), calls=%async_computation.1 | async-start | bytes 524288 | tf_op jit(solution)/shard_map/while/body/eval_jaxpr/psum | solution.py:11
  1109.7 46.2 %all-reduce.9.cloned.1.call-start = ((), (), s32[]{:S(2)}) async-start(), calls=%async_computation.2 | async-start | bytes 524288 | tf_op jit(solution)/shard_map/while/body/eval_jaxpr/psum | solution.py:112
  1109.9 7.3 collective-permute-start
  1113.1 131.8 %all-reduce.7.cloned.1.call-start = ((), (), s32[]{:S(2)}) async-start(), calls=%async_computation.1 | async-start | bytes 524288 | tf_op jit(solution)/shard_map/while/body/eval_jaxpr/psum | solution.py:11
  1244.9 50.7 %all-reduce.9.cloned.1.call-start = ((), (), s32[]{:S(2)}) async-start(), calls=%async_computation.2 | async-start | bytes 524288 | tf_op jit(solution)/shard_map/while/body/eval_jaxpr/psum | solution.py:112
  1245.1 9.1 collective-permute-start
  1250.2 133.2 %all-reduce.7.cloned.1.call-start = ((), (), s32[]{:S(2)}) async-start(), calls=%async_computation.1 | async-start | bytes 524288 | tf_op jit(solution)/shard_map/while/body/eval_jaxpr/psum | solution.py:11
  1383.4 48.7 %all-reduce.9.cloned.1.call-start = ((), (), s32[]{:S(2)}) async-start(), calls=%async_computation.2 | async-start | bytes 524288 | tf_op jit(solution)/shard_map/while/body/eval_jaxpr/psum | solution.py:112
  1383.5 8.1 collective-permute-start
  1387.7 130.7 %all-reduce.7.cloned.1.call-start = ((), (), s32[]{:S(2)}) async-start(), calls=%async_computation.1 | async-start | bytes 524288 | tf_op jit(solution)/shard_map/while/body/eval_jaxpr/psum | solution.py:11
  1518.4 49.7 %all-reduce.9.cloned.1.call-start = ((), (), s32[]{:S(2)}) async-start(), calls=%async_computation.2 | async-start | bytes 524288 | tf_op jit(solution)/shard_map/while/body/eval_jaxpr/psum | solution.py:112
  1518.6 8.1 collective-permute-start
  1522.7 132.2 %all-reduce.7.cloned.1.call-start = ((), (), s32[]{:S(2)}) async-start(), calls=%async_computation.1 | async-start | bytes 524288 | tf_op jit(solution)/shard_map/while/body/eval_jaxpr/psum | solution.py:11
  1656.0 46.0 %all-reduce.9.cloned.1.call-start = ((), (), s32[]{:S(2)}) async-start(), calls=%async_computation.2 | async-start | bytes 524288 | tf_op jit(solution)/shard_map/while/body/eval_jaxpr/psum | solution.py:112
  1656.1 7.3 collective-permute-start
  1659.3 131.6 %all-reduce.7.cloned.1.call-start = ((), (), s32[]{:S(2)}) async-start(), calls=%async_computation.1 | async-start | bytes 524288 | tf_op jit(solution)/shard_map/while/body/eval_jaxpr/psum | solution.py:11
  1791.0 50.6 %all-reduce.9.cloned.1.call-start = ((), (), s32[]{:S(2)}) async-start(), calls=%async_computation.2 | async-start | bytes 524288 | tf_op jit(solution)/shard_map/while/body/eval_jaxpr/psum | solution.py:112
  1791.2 9.1 collective-permute-start
  1796.3 133.1 %all-reduce.7.cloned.1.call-start = ((), (), s32[]{:S(2)}) async-start(), calls=%async_computation.1 | async-start | bytes 524288 | tf_op jit(solution)/shard_map/while/body/eval_jaxpr/psum | solution.py:11
  1929.5 48.7 %all-reduce.9.cloned.1.call-start = ((), (), s32[]{:S(2)}) async-start(), calls=%async_computation.2 | async-start | bytes 524288 | tf_op jit(solution)/shard_map/while/body/eval_jaxpr/psum | solution.py:112
  1929.6 9.9 collective-permute-start
  1939.4 125.0 %all-reduce.7.cloned.1.call-start = ((), (), s32[]{:S(2)}) async-start(), calls=%async_computation.1 | async-start | bytes 524288 | tf_op jit(solution)/shard_map/while/body/eval_jaxpr/psum | solution.py:11
  2064.5 86.0 %all-reduce.9.cloned.1.call-start = ((), (), s32[]{:S(2)}) async-start(), calls=%async_computation.2 | async-start | bytes 524288 | tf_op jit(solution)/shard_map/while/body/eval_jaxpr/psum | solution.py:112
  2064.7 19.9 collective-permute-start
  2074.5 125.8 %all-reduce.7.cloned.1.call-start = ((), (), s32[]{:S(2)}) async-start(), calls=%async_computation.1 | async-start | bytes 524288 | tf_op jit(solution)/shard_map/while/body/eval_jaxpr/psum | solution.py:11
  (16 other events, 22.0 us)
Sparse Core Ops, SparseCore 0:
  35.2 117.8 all-reduce.4
  158.6 45.2 all-reduce.8
  207.6 84.0 all-reduce.6
  296.2 44.2 all-reduce.8
  343.9 82.7 all-reduce.6
  431.2 45.2 all-reduce.8
  480.1 83.1 all-reduce.6
  567.8 42.4 all-reduce.8
  614.0 85.3 all-reduce.6
  704.8 45.2 all-reduce.8
  753.7 84.0 all-reduce.6
  847.9 38.5 all-reduce.8
  890.2 82.6 all-reduce.6
  977.3 44.9 all-reduce.8
  1058.9 49.7 all-reduce.6
  1113.2 42.6 all-reduce.8
  1159.4 85.4 all-reduce.6
  1250.3 45.2 all-reduce.8
  1299.2 84.0 all-reduce.6
  1387.8 44.2 all-reduce.8
  1435.7 82.6 all-reduce.6
  1522.8 45.2 all-reduce.8
  1571.7 83.1 all-reduce.6
  1659.5 42.4 all-reduce.8
  1705.6 85.3 all-reduce.6
  1796.4 45.2 all-reduce.8
  1845.1 84.2 all-reduce.6
  1939.6 38.5 all-reduce.8
  1981.8 82.6 all-reduce.6
  2074.7 45.0 all-reduce.8
  2150.6 49.7 all-reduce.6
where the time goes:
time: 2220 us
  waiting for transfers between devices  1920 us (86%)
  other arithmetic  111 us (5%)
  local copies, waits for them, and re-layouts  84.6 us (4%)
  starting transfers between devices  53 us (2%)
  matrix products  32.1 us (1%)
    psum x16, waiting for transfers between devices, broadcast(): return lax.psum(jnp.where(mine, value, jnp.zeros_like(value)), axis)  1340 us
    psum x15, waiting for transfers between devices, sweep_step(): next_sum = lax.psum(next_partial, 'row')  512 us
    another operation x10, other arithmetic, solve_here(): lax.linalg.triangular_solve(diagonal, right_side, left_side=True, lower=T...  83 us
    ppermute x15, waiting for transfers between devices, from_behind(): lax.ppermute(value, axis, [(i, (i + by) % size) for i in range(size)])  68.5 us
    ppermute x15, starting transfers between devices, from_behind(): lax.ppermute(value, axis, [(i, (i + by) % size) for i in range(size)])  51.7 us
  transfers between devices with their start and end apart: 46, of which 42 were waited for; matrix products, arithmetic and copies ran while one was open for 8% of the time, Pallas kernels for 0%

commit v1 on v0

--- a/solution.py
+++ b/solution.py
@@ -109,7 +109,11 @@
         moved_term = from_behind(fresh_term, "row", -1)
         following = jnp.maximum(target - 1, 0)
         next_partial = column_partial(rhs_local, following, source)
-        next_sum = lax.psum(next_partial, "row")
+        next_sum = next_partial
+        for hop in (1, 2):
+            next_sum = next_sum + lax.ppermute(
+                next_sum, "row", [(dev, dev ^ hop) for dev in range(4)]
+            )
         carried = advance(target_block(target) - early_sum - moved_term, target, carried)
         return (carried, next_sum)
 

time: 2220 us -> 2300 us (1.036)
  starting transfers between devices: 53 us -> 99 us
  waiting for transfers between devices: 1920 us -> 1950 us
  other arithmetic: 111 us -> 139 us
  local copies, waits for them, and re-layouts: 84.6 us -> 60.8 us
    psum x15 -> x0, waiting for transfers between devices: 512 us -> none  [sweep_step(): next_sum = lax.psum(next_partial, 'row')]
    psum x16, waiting for transfers between devices: 1340 us -> 1830 us  [broadcast(): return lax.psum(jnp.where(mine, value, jnp.zeros_like(value)), axis)]
    ppermute x0 -> x30, starting transfers between devices: none -> 47.2 us  [sweep_step(): lax.ppermute(next_sum, 'row', [(dev, dev ^ hop) for dev in range(4)])]
    ppermute x0 -> x30, waiting for transfers between devices: none -> 44.8 us  [sweep_step(): lax.ppermute(next_sum, 'row', [(dev, dev ^ hop) for dev in range(4)])]
    add x0 -> x30, other arithmetic: none -> 26 us  [sweep_step(): next_sum + lax.ppermute(next_sum, 'row', [(dev, dev ^ hop) for dev in ran...]
    while x45 -> x15, local copies, waits for them, and re-layouts: 25 us -> 0.27 us
  transfers between devices with their start and end apart: 46 -> 61, of which waited for: 42 -> 43; matrix products, arithmetic and copies ran while one was open for 8% -> 8% of each run, Pallas kernels for 0% -> 0%
where the time goes in v1:
time: 2300 us
  waiting for transfers between devices  1950 us (85%)
  other arithmetic  139 us (6%)
  starting transfers between devices  99 us (4%)
  local copies, waits for them, and re-layouts  60.8 us (3%)
  matrix products  38.6 us (2%)
    psum x16, waiting for transfers between devices, broadcast(): return lax.psum(jnp.where(mine, value, jnp.zeros_like(value)), axis)  1830 us
    another operation x10, other arithmetic, solve_here(): lax.linalg.triangular_solve(diagonal, right_side, left_side=True, lower=T...  84.2 us
    ppermute x15, waiting for transfers between devices, from_behind(): lax.ppermute(value, axis, [(i, (i + by) % size) for i in range(size)])  74.7 us
    ppermute x15, starting transfers between devices, from_behind(): lax.ppermute(value, axis, [(i, (i + by) % size) for i in range(size)])  51.7 us
    ppermute x30, starting transfers between devices, sweep_step(): lax.ppermute(next_sum, 'row', [(dev, dev ^ hop) for dev in range(4)])  47.2 us
  transfers between devices with their start and end apart: 61, of which 43 were waited for; matrix products, arithmetic and copies ran while one was open for 8% of the time, Pallas kernels for 0%

profile of v1, /device:TPU:0, one launch (start us, length us, event | category | flops | bytes accessed | tf_op | source)
XLA Modules:
  0.0 2300.6 jit_solution(567687843818260156)
XLA Ops:
  7.3 9.9 copy.12
  17.2 7.3 copy.11
  24.4 9.6 convert_select_fusion
  35.9 117.0 %all-reduce.4.cloned.1.call-done = f32[512,128]{1,0:T(8,128)} async-done(((f32[512,128]{1,0:T(8,128)}), f32[512,128]{1,0:T(8,128)}) %all-reduce.4.cloned.1.call-update) | async-done | bytes 262160 | tf_op jit(solution)/shard_map/psum | solution.py:11
  153.0 2130.2 %while.29 = (s32[]{:T(128)}, f32[4,512,128]{2,1,0:T(8,128)S(1)}, f32[512,128]{1,0:T(8,128)}, s32[]{:T(128)}, s32[]{:T(128)}, /*index=5*/f32[4,2,512,512]{2,3,0,1...) while((s32[]{:T(128)}, f32[4,512,128]{2,1,0:T(8,128)S(1)}, ...), condition=%wide.region_11.13_spmd.clone.clone.clone, body=%wide.region_3.12_spmd.clone.clone.clone.sunk | while | flops 2266611712 | bytes 56102800 | solution.py:120
  157.7 6.5 collective-permute-done
  170.4 125.8 %all-reduce.6.cloned.1.call-done = f32[512,128]{1,0:T(8,128)} async-done(((f32[512,128]{1,0:T(8,128)}), f32[512,128]{1,0:T(8,128)}) %all-reduce.6.cloned.1.call-update) | async-done | bytes 262160 | tf_op jit(solution)/shard_map/while/body/eval_jaxpr/psum | solution.py:11
  300.5 6.5 collective-permute-done
  314.4 122.0 %all-reduce.6.cloned.1.call-done = f32[512,128]{1,0:T(8,128)} async-done(((f32[512,128]{1,0:T(8,128)}), f32[512,128]{1,0:T(8,128)}) %all-reduce.6.cloned.1.call-update) | async-done | bytes 262160 | tf_op jit(solution)/shard_map/while/body/eval_jaxpr/psum | solution.py:11
  440.9 6.5 collective-permute-done
  453.8 124.8 %all-reduce.6.cloned.1.call-done = f32[512,128]{1,0:T(8,128)} async-done(((f32[512,128]{1,0:T(8,128)}), f32[512,128]{1,0:T(8,128)}) %all-reduce.6.cloned.1.call-update) | async-done | bytes 262160 | tf_op jit(solution)/shard_map/while/body/eval_jaxpr/psum | solution.py:11
  583.0 6.6 collective-permute-done
  595.9 123.9 %all-reduce.6.cloned.1.call-done = f32[512,128]{1,0:T(8,128)} async-done(((f32[512,128]{1,0:T(8,128)}), f32[512,128]{1,0:T(8,128)}) %all-reduce.6.cloned.1.call-update) | async-done | bytes 262160 | tf_op jit(solution)/shard_map/while/body/eval_jaxpr/psum | solution.py:11
  738.7 124.9 %all-reduce.6.cloned.1.call-done = f32[512,128]{1,0:T(8,128)} async-done(((f32[512,128]{1,0:T(8,128)}), f32[512,128]{1,0:T(8,128)}) %all-reduce.6.cloned.1.call-update) | async-done | bytes 262160 | tf_op jit(solution)/shard_map/while/body/eval_jaxpr/psum | solution.py:11
  867.8 5.7 conditional.19
  867.8 5.7 fusion.11
  875.3 4.7 collective-permute-done.1
  881.2 122.7 %all-reduce.6.cloned.1.call-done = f32[512,128]{1,0:T(8,128)} async-done(((f32[512,128]{1,0:T(8,128)}), f32[512,128]{1,0:T(8,128)}) %all-reduce.6.cloned.1.call-update) | async-done | bytes 262160 | tf_op jit(solution)/shard_map/while/body/eval_jaxpr/psum | solution.py:11
  1008.2 12.2 collective-permute-start.1
  1025.1 69.9 %conditional.18 = (f32[512,128]{1,0:T(8,128)S(1)}) conditional(s32[]{:T(128)} %convert_element_type.71, () %tuple.154, (s32[]{:T(128)}, s32[]{:T(128)}, f32[4,2,512,512]{2,3,0,1:T(8,128)}, s32[]{:T(128)}, pred[]{:T(512)}, /*index=5*/pred[]{:T(512)}, s32[]{:T(128)}, f32[2,512,128]{2,1,0:T(8,128)}, s32[]{:T(128)}, f32[512,128]{1,0:T(8,128)S(1)}, ...), branch_computations={%region_6.7_spmd, %region_7.8_spmd} | conditional | flops 252756000 | bytes 23857272 | solution.py:76
  1025.8 10.0 copy.8
  1037.1 10.5 while.28
  1047.6 40.7 %custom-call.6 = f32[4,128,128]{1,2,0:T(8,128)} custom-call(f32[4,128,128]{2,1,0:T(8,128)} %get-tuple-element.591), custom_call_target="InvertDiagBlocksLowerTriangular" | custom-call | tf_op jit(solution)/shard_map/while/body/eval_jaxpr/cond/branch_1_fun/triangular_solve/custom-call.1 | solution.py:72
  1096.8 48.8 %all-reduce.6.cloned.1.call-done = f32[512,128]{1,0:T(8,128)} async-done(((f32[512,128]{1,0:T(8,128)}), f32[512,128]{1,0:T(8,128)}) %all-reduce.6.cloned.1.call-update) | async-done | bytes 262160 | tf_op jit(solution)/shard_map/while/body/eval_jaxpr/psum | solution.py:11
  1150.0 6.6 collective-permute-done
  1162.9 124.2 %all-reduce.6.cloned.1.call-done = f32[512,128]{1,0:T(8,128)} async-done(((f32[512,128]{1,0:T(8,128)}), f32[512,128]{1,0:T(8,128)}) %all-reduce.6.cloned.1.call-update) | async-done | bytes 262160 | tf_op jit(solution)/shard_map/while/body/eval_jaxpr/psum | solution.py:11
  1292.4 6.5 collective-permute-done
  1305.1 125.8 %all-reduce.6.cloned.1.call-done = f32[512,128]{1,0:T(8,128)} async-done(((f32[512,128]{1,0:T(8,128)}), f32[512,128]{1,0:T(8,128)}) %all-reduce.6.cloned.1.call-update) | async-done | bytes 262160 | tf_op jit(solution)/shard_map/while/body/eval_jaxpr/psum | solution.py:11
  1435.3 6.5 collective-permute-done
  1449.2 122.0 %all-reduce.6.cloned.1.call-done = f32[512,128]{1,0:T(8,128)} async-done(((f32[512,128]{1,0:T(8,128)}), f32[512,128]{1,0:T(8,128)}) %all-reduce.6.cloned.1.call-update) | async-done | bytes 262160 | tf_op jit(solution)/shard_map/while/body/eval_jaxpr/psum | solution.py:11
  1575.6 6.5 collective-permute-done
  1588.6 124.8 %all-reduce.6.cloned.1.call-done = f32[512,128]{1,0:T(8,128)} async-done(((f32[512,128]{1,0:T(8,128)}), f32[512,128]{1,0:T(8,128)}) %all-reduce.6.cloned.1.call-update) | async-done | bytes 262160 | tf_op jit(solution)/shard_map/while/body/eval_jaxpr/psum | solution.py:11
  1717.7 6.6 collective-permute-done
  1730.7 124.0 %all-reduce.6.cloned.1.call-done = f32[512,128]{1,0:T(8,128)} async-done(((f32[512,128]{1,0:T(8,128)}), f32[512,128]{1,0:T(8,128)}) %all-reduce.6.cloned.1.call-update) | async-done | bytes 262160 | tf_op jit(solution)/shard_map/while/body/eval_jaxpr/psum | solution.py:11
  1873.5 124.9 %all-reduce.6.cloned.1.call-done = f32[512,128]{1,0:T(8,128)} async-done(((f32[512,128]{1,0:T(8,128)}), f32[512,128]{1,0:T(8,128)}) %all-reduce.6.cloned.1.call-update) | async-done | bytes 262160 | tf_op jit(solution)/shard_map/while/body/eval_jaxpr/psum | solution.py:11
  2002.6 5.7 conditional.19
  2002.6 5.7 fusion.11
  2010.1 4.7 collective-permute-done.1
  2016.1 122.7 %all-reduce.6.cloned.1.call-done = f32[512,128]{1,0:T(8,128)} async-done(((f32[512,128]{1,0:T(8,128)}), f32[512,128]{1,0:T(8,128)}) %all-reduce.6.cloned.1.call-update) | async-done | bytes 262160 | tf_op jit(solution)/shard_map/while/body/eval_jaxpr/psum | solution.py:11
  2143.0 5.7 conditional.19
  2143.0 5.7 fusion.11
  2148.7 12.2 collective-permute-start.1
  2160.9 69.9 %conditional.18 = (f32[512,128]{1,0:T(8,128)S(1)}) conditional(s32[]{:T(128)} %convert_element_type.71, () %tuple.154, (s32[]{:T(128)}, s32[]{:T(128)}, f32[4,2,512,512]{2,3,0,1:T(8,128)}, s32[]{:T(128)}, pred[]{:T(512)}, /*index=5*/pred[]{:T(512)}, s32[]{:T(128)}, f32[2,512,128]{2,1,0:T(8,128)}, s32[]{:T(128)}, f32[512,128]{1,0:T(8,128)S(1)}, ...), branch_computations={%region_6.7_spmd, %region_7.8_spmd} | conditional | flops 252756000 | bytes 23857272 | solution.py:76
  2161.7 10.0 copy.8
  2173.0 10.5 while.28
  2183.5 40.7 %custom-call.6 = f32[4,128,128]{1,2,0:T(8,128)} custom-call(f32[4,128,128]{2,1,0:T(8,128)} %get-tuple-element.591), custom_call_target="InvertDiagBlocksLowerTriangular" | custom-call | tf_op jit(solution)/shard_map/while/body/eval_jaxpr/cond/branch_1_fun/triangular_solve/custom-call.1 | solution.py:72
  2232.7 48.8 %all-reduce.6.cloned.1.call-done = f32[512,128]{1,0:T(8,128)} async-done(((f32[512,128]{1,0:T(8,128)}), f32[512,128]{1,0:T(8,128)}) %all-reduce.6.cloned.1.call-update) | async-done | bytes 262160 | tf_op jit(solution)/shard_map/while/body/eval_jaxpr/psum | solution.py:11
  2283.2 10.9 fusion.55
  (369 shorter events, 209.3 us)
Async XLA Ops:
  7.2 145.7 %all-reduce.4.cloned.1.call-start = ((), (), s32[]{:S(2)}) async-start(), calls=%async_computation | async-start | bytes 524288 | tf_op jit(solution)/shard_map/psum | solution.py:11
  153.0 143.1 %all-reduce.6.cloned.1.call-start = ((), (), s32[]{:S(2)}) async-start(), calls=%async_computation.1 | async-start | bytes 524288 | tf_op jit(solution)/shard_map/while/body/eval_jaxpr/psum | solution.py:11
  153.2 11.0 collective-permute-start
  157.5 10.3 collective-permute-start.1
  168.9 127.3 %collective-permute-start.2 = (f32[512,128]{1,0:T(8,128)S(1)}, f32[512,128]{1,0:T(8,128)S(1)}, u32[]{:S(2)}, u32[]{:S(2)}) collective-permute-start(f32[512,128]{1,0:T(8,128)S(1)} %add.341), channel_id=1, source_target_pairs={{0,16},{8,24},{16,0},{24,8},{1,17},{9,25},{17,1},{25,9},{2,18},{10... | collective-permute-start | bytes 786440 | tf_op jit(solution)/shard_map/while/body/eval_jaxpr/ppermute | solution.py:114
  297.0 139.5 %all-reduce.6.cloned.1.call-start = ((), (), s32[]{:S(2)}) async-start(), calls=%async_computation.1 | async-start | bytes 524288 | tf_op jit(solution)/shard_map/while/body/eval_jaxpr/psum | solution.py:11
  300.4 10.3 collective-permute-start.1
  311.7 124.8 %collective-permute-start.2 = (f32[512,128]{1,0:T(8,128)S(1)}, f32[512,128]{1,0:T(8,128)S(1)}, u32[]{:S(2)}, u32[]{:S(2)}) collective-permute-start(f32[512,128]{1,0:T(8,128)S(1)} %add.341), channel_id=1, source_target_pairs={{0,16},{8,24},{16,0},{24,8},{1,17},{9,25},{17,1},{25,9},{2,18},{10... | collective-permute-start | bytes 786440 | tf_op jit(solution)/shard_map/while/body/eval_jaxpr/ppermute | solution.py:114
  437.3 141.3 %all-reduce.6.cloned.1.call-start = ((), (), s32[]{:S(2)}) async-start(), calls=%async_computation.1 | async-start | bytes 524288 | tf_op jit(solution)/shard_map/while/body/eval_jaxpr/psum | solution.py:11
  440.7 10.3 collective-permute-start.1
  452.1 127.5 %collective-permute-start.2 = (f32[512,128]{1,0:T(8,128)S(1)}, f32[512,128]{1,0:T(8,128)S(1)}, u32[]{:S(2)}, u32[]{:S(2)}) collective-permute-start(f32[512,128]{1,0:T(8,128)S(1)} %add.341), channel_id=1, source_target_pairs={{0,16},{8,24},{16,0},{24,8},{1,17},{9,25},{17,1},{25,9},{2,18},{10... | collective-permute-start | bytes 786440 | tf_op jit(solution)/shard_map/while/body/eval_jaxpr/ppermute | solution.py:114
  580.3 139.5 %all-reduce.6.cloned.1.call-start = ((), (), s32[]{:S(2)}) async-start(), calls=%async_computation.1 | async-start | bytes 524288 | tf_op jit(solution)/shard_map/while/body/eval_jaxpr/psum | solution.py:11
  582.8 10.6 collective-permute-start.1
  594.4 125.5 %collective-permute-start.2 = (f32[512,128]{1,0:T(8,128)S(1)}, f32[512,128]{1,0:T(8,128)S(1)}, u32[]{:S(2)}, u32[]{:S(2)}) collective-permute-start(f32[512,128]{1,0:T(8,128)S(1)} %add.341), channel_id=1, source_target_pairs={{0,16},{8,24},{16,0},{24,8},{1,17},{9,25},{17,1},{25,9},{2,18},{10... | collective-permute-start | bytes 786440 | tf_op jit(solution)/shard_map/while/body/eval_jaxpr/ppermute | solution.py:114
  720.7 142.9 %all-reduce.6.cloned.1.call-start = ((), (), s32[]{:S(2)}) async-start(), calls=%async_computation.1 | async-start | bytes 524288 | tf_op jit(solution)/shard_map/while/body/eval_jaxpr/psum | solution.py:11
  725.0 10.2 collective-permute-start.1
  736.2 127.4 %collective-permute-start.2 = (f32[512,128]{1,0:T(8,128)S(1)}, f32[512,128]{1,0:T(8,128)S(1)}, u32[]{:S(2)}, u32[]{:S(2)}) collective-permute-start(f32[512,128]{1,0:T(8,128)S(1)} %add.341), channel_id=1, source_target_pairs={{0,16},{8,24},{16,0},{24,8},{1,17},{9,25},{17,1},{25,9},{2,18},{10... | collective-permute-start | bytes 786440 | tf_op jit(solution)/shard_map/while/body/eval_jaxpr/ppermute | solution.py:114
  864.4 139.5 %all-reduce.6.cloned.1.call-start = ((), (), s32[]{:S(2)}) async-start(), calls=%async_computation.1 | async-start | bytes 524288 | tf_op jit(solution)/shard_map/while/body/eval_jaxpr/psum | solution.py:11
  881.0 122.9 %collective-permute-start.2 = (f32[512,128]{1,0:T(8,128)S(1)}, f32[512,128]{1,0:T(8,128)S(1)}, u32[]{:S(2)}, u32[]{:S(2)}) collective-permute-start(f32[512,128]{1,0:T(8,128)S(1)} %add.341), channel_id=1, source_target_pairs={{0,16},{8,24},{16,0},{24,8},{1,17},{9,25},{17,1},{25,9},{2,18},{10... | collective-permute-start | bytes 786440 | tf_op jit(solution)/shard_map/while/body/eval_jaxpr/ppermute | solution.py:114
  1004.7 140.9 %all-reduce.6.cloned.1.call-start = ((), (), s32[]{:S(2)}) async-start(), calls=%async_computation.1 | async-start | bytes 524288 | tf_op jit(solution)/shard_map/while/body/eval_jaxpr/psum | solution.py:11
  1004.8 20.3 collective-permute-start
  1008.2 87.5 %collective-permute-start.1 = (f32[512,128]{1,0:T(8,128)S(1)}, f32[512,128]{1,0:T(8,128)}, u32[]{:S(2)}, u32[]{:S(2)}) collective-permute-start(f32[512,128]{1,0:T(8,128)S(1)} %get-tuple-element.852), channel_id=1, source_target_pairs={{0,8},{8,0},{16,24},{24,16},{1,9},{9,1},{17,25},{25,17},{2,10},{10... | collective-permute-start | bytes 786440 | tf_op jit(solution)/shard_map/while/body/eval_jaxpr/ppermute | solution.py:114
  1096.7 49.9 %collective-permute-start.2 = (f32[512,128]{1,0:T(8,128)S(1)}, f32[512,128]{1,0:T(8,128)S(1)}, u32[]{:S(2)}, u32[]{:S(2)}) collective-permute-start(f32[512,128]{1,0:T(8,128)S(1)} %add.341), channel_id=1, source_target_pairs={{0,16},{8,24},{16,0},{24,8},{1,17},{9,25},{17,1},{25,9},{2,18},{10... | collective-permute-start | bytes 786440 | tf_op jit(solution)/shard_map/while/body/eval_jaxpr/ppermute | solution.py:114
  1147.4 139.8 %all-reduce.6.cloned.1.call-start = ((), (), s32[]{:S(2)}) async-start(), calls=%async_computation.1 | async-start | bytes 524288 | tf_op jit(solution)/shard_map/while/body/eval_jaxpr/psum | solution.py:11
  1149.9 10.6 collective-permute-start.1
  1161.4 125.8 %collective-permute-start.2 = (f32[512,128]{1,0:T(8,128)S(1)}, f32[512,128]{1,0:T(8,128)S(1)}, u32[]{:S(2)}, u32[]{:S(2)}) collective-permute-start(f32[512,128]{1,0:T(8,128)S(1)} %add.341), channel_id=1, source_target_pairs={{0,16},{8,24},{16,0},{24,8},{1,17},{9,25},{17,1},{25,9},{2,18},{10... | collective-permute-start | bytes 786440 | tf_op jit(solution)/shard_map/while/body/eval_jaxpr/ppermute | solution.py:114
  1287.9 143.0 %all-reduce.6.cloned.1.call-start = ((), (), s32[]{:S(2)}) async-start(), calls=%async_computation.1 | async-start | bytes 524288 | tf_op jit(solution)/shard_map/while/body/eval_jaxpr/psum | solution.py:11
  1287.9 11.0 collective-permute-start
  1292.3 10.3 collective-permute-start.1
  1303.6 127.3 %collective-permute-start.2 = (f32[512,128]{1,0:T(8,128)S(1)}, f32[512,128]{1,0:T(8,128)S(1)}, u32[]{:S(2)}, u32[]{:S(2)}) collective-permute-start(f32[512,128]{1,0:T(8,128)S(1)} %add.341), channel_id=1, source_target_pairs={{0,16},{8,24},{16,0},{24,8},{1,17},{9,25},{17,1},{25,9},{2,18},{10... | collective-permute-start | bytes 786440 | tf_op jit(solution)/shard_map/while/body/eval_jaxpr/ppermute | solution.py:114
  1431.7 139.5 %all-reduce.6.cloned.1.call-start = ((), (), s32[]{:S(2)}) async-start(), calls=%async_computation.1 | async-start | bytes 524288 | tf_op jit(solution)/shard_map/while/body/eval_jaxpr/psum | solution.py:11
  1435.2 10.3 collective-permute-start.1
  1446.5 124.8 %collective-permute-start.2 = (f32[512,128]{1,0:T(8,128)S(1)}, f32[512,128]{1,0:T(8,128)S(1)}, u32[]{:S(2)}, u32[]{:S(2)}) collective-permute-start(f32[512,128]{1,0:T(8,128)S(1)} %add.341), channel_id=1, source_target_pairs={{0,16},{8,24},{16,0},{24,8},{1,17},{9,25},{17,1},{25,9},{2,18},{10... | collective-permute-start | bytes 786440 | tf_op jit(solution)/shard_map/while/body/eval_jaxpr/ppermute | solution.py:114
  1572.1 141.3 %all-reduce.6.cloned.1.call-start = ((), (), s32[]{:S(2)}) async-start(), calls=%async_computation.1 | async-start | bytes 524288 | tf_op jit(solution)/shard_map/while/body/eval_jaxpr/psum | solution.py:11
  1575.5 10.3 collective-permute-start.1
  1586.8 127.5 %collective-permute-start.2 = (f32[512,128]{1,0:T(8,128)S(1)}, f32[512,128]{1,0:T(8,128)S(1)}, u32[]{:S(2)}, u32[]{:S(2)}) collective-permute-start(f32[512,128]{1,0:T(8,128)S(1)} %add.341), channel_id=1, source_target_pairs={{0,16},{8,24},{16,0},{24,8},{1,17},{9,25},{17,1},{25,9},{2,18},{10... | collective-permute-start | bytes 786440 | tf_op jit(solution)/shard_map/while/body/eval_jaxpr/ppermute | solution.py:114
  1715.1 139.5 %all-reduce.6.cloned.1.call-start = ((), (), s32[]{:S(2)}) async-start(), calls=%async_computation.1 | async-start | bytes 524288 | tf_op jit(solution)/shard_map/while/body/eval_jaxpr/psum | solution.py:11
  1717.6 10.6 collective-permute-start.1
  1729.1 125.6 %collective-permute-start.2 = (f32[512,128]{1,0:T(8,128)S(1)}, f32[512,128]{1,0:T(8,128)S(1)}, u32[]{:S(2)}, u32[]{:S(2)}) collective-permute-start(f32[512,128]{1,0:T(8,128)S(1)} %add.341), channel_id=1, source_target_pairs={{0,16},{8,24},{16,0},{24,8},{1,17},{9,25},{17,1},{25,9},{2,18},{10... | collective-permute-start | bytes 786440 | tf_op jit(solution)/shard_map/while/body/eval_jaxpr/ppermute | solution.py:114
  1855.5 143.0 %all-reduce.6.cloned.1.call-start = ((), (), s32[]{:S(2)}) async-start(), calls=%async_computation.1 | async-start | bytes 524288 | tf_op jit(solution)/shard_map/while/body/eval_jaxpr/psum | solution.py:11
  1859.8 10.2 collective-permute-start.1
  1871.0 127.4 %collective-permute-start.2 = (f32[512,128]{1,0:T(8,128)S(1)}, f32[512,128]{1,0:T(8,128)S(1)}, u32[]{:S(2)}, u32[]{:S(2)}) collective-permute-start(f32[512,128]{1,0:T(8,128)S(1)} %add.341), channel_id=1, source_target_pairs={{0,16},{8,24},{16,0},{24,8},{1,17},{9,25},{17,1},{25,9},{2,18},{10... | collective-permute-start | bytes 786440 | tf_op jit(solution)/shard_map/while/body/eval_jaxpr/ppermute | solution.py:114
  1999.2 139.5 %all-reduce.6.cloned.1.call-start = ((), (), s32[]{:S(2)}) async-start(), calls=%async_computation.1 | async-start | bytes 524288 | tf_op jit(solution)/shard_map/while/body/eval_jaxpr/psum | solution.py:11
  2015.9 122.9 %collective-permute-start.2 = (f32[512,128]{1,0:T(8,128)S(1)}, f32[512,128]{1,0:T(8,128)S(1)}, u32[]{:S(2)}, u32[]{:S(2)}) collective-permute-start(f32[512,128]{1,0:T(8,128)S(1)} %add.341), channel_id=1, source_target_pairs={{0,16},{8,24},{16,0},{24,8},{1,17},{9,25},{17,1},{25,9},{2,18},{10... | collective-permute-start | bytes 786440 | tf_op jit(solution)/shard_map/while/body/eval_jaxpr/ppermute | solution.py:114
  2139.6 141.9 %all-reduce.6.cloned.1.call-start = ((), (), s32[]{:S(2)}) async-start(), calls=%async_computation.1 | async-start | bytes 524288 | tf_op jit(solution)/shard_map/while/body/eval_jaxpr/psum | solution.py:11
  2139.6 21.3 collective-permute-start
  2148.7 82.9 %collective-permute-start.1 = (f32[512,128]{1,0:T(8,128)S(1)}, f32[512,128]{1,0:T(8,128)}, u32[]{:S(2)}, u32[]{:S(2)}) collective-permute-start(f32[512,128]{1,0:T(8,128)S(1)} %get-tuple-element.852), channel_id=1, source_target_pairs={{0,8},{8,0},{16,24},{24,16},{1,9},{9,1},{17,25},{25,17},{2,10},{10... | collective-permute-start | bytes 786440 | tf_op jit(solution)/shard_map/while/body/eval_jaxpr/ppermute | solution.py:114
  2232.5 49.9 %collective-permute-start.2 = (f32[512,128]{1,0:T(8,128)S(1)}, f32[512,128]{1,0:T(8,128)S(1)}, u32[]{:S(2)}, u32[]{:S(2)}) collective-permute-start(f32[512,128]{1,0:T(8,128)S(1)} %add.341), channel_id=1, source_target_pairs={{0,16},{8,24},{16,0},{24,8},{1,17},{9,25},{17,1},{25,9},{2,18},{10... | collective-permute-start | bytes 786440 | tf_op jit(solution)/shard_map/while/body/eval_jaxpr/ppermute | solution.py:114
  (18 other events, 2425.0 us)
Sparse Core Ops, SparseCore 0:
  35.1 117.7 all-reduce.3
  165.1 130.9 all-reduce.5
  308.0 128.4 all-reduce.5
  448.3 130.1 all-reduce.5
  590.5 129.2 all-reduce.5
  730.7 132.8 all-reduce.5
  875.4 128.4 all-reduce.5
  1095.8 49.7 all-reduce.5
  1157.6 129.5 all-reduce.5
  1299.9 130.9 all-reduce.5
  1442.8 128.4 all-reduce.5
  1583.1 130.1 all-reduce.5
  1725.3 129.3 all-reduce.5
  1865.5 132.8 all-reduce.5
  2010.3 128.4 all-reduce.5
  2231.7 49.7 all-reduce.5
